TPU v7x, 256 devices: a whole 4x4x8 slice. The times are simulated.
256 devices in a mesh: prow: 32 (over x, z), pcol: 8 (over y, core).
Axes of the slice: x: 4, y: 4, z: 8, core: 2. Of those that a mesh axis runs over, the one named last changes fastest.
Arguments:
- inverse_pool: float32 [12288, 12288], P('prow', 'pcol'), may hold values from -6 to 6
- panel_one: float32 [12288, 512], P(('prow', 'pcol')), may hold values from -0.0625 to 0.0625
- panel_two: float32 [12288, 512], P(('prow', 'pcol')), may hold values from -0.078125 to 0.078125
- upper_two: float32 [512, 512], replicated, may hold values from -0.25 to 0.25
- lower_one: float32 [512, 512], replicated, as said below
- lower_two: float32 [512, 512], replicated, as said below
- list_one: int32 [72], replicated, may hold values from 0 to 95, as said below
- list_two: int32 [48], replicated, may hold values from 0 to 95, as said below
Outputs:
- first_offdiag: float32 [12288, 512], P(('prow', 'pcol'))
- first_diag: float32 [512, 512], replicated
- second_offdiag: float32 [12288, 512], P(('prow', 'pcol'))
- second_coupling: float32 [512, 512], replicated
- second_diag: float32 [512, 512], replicated
Inputs may be any that keep to these rules, and one draw needn't show every extreme that they name: `list_one`: distinct block numbers, among them 0, 48 and 95. `list_two`: distinct block numbers, each of which is also in list_one, among them 0, 48 and 95. `lower_one`: lower triangular with a diagonal of 1 to 1.5. `lower_two`: lower triangular with a diagonal of 1 to 1.5.
All inputs are finite; a program needn't handle non-finite values.
Results may differ from a plain program's by a relative error of at most 0.000073.
Values sent between devices are 32-bit elements; how exact they have to be, the bound alone decides.
No kernel may reach another device: no remote copies, remote signals or barrier semaphores. Data moves between devices by JAX's collectives and lax.ppermute only.
A program may use at most 64 MiB of HBM per device.

v0:
```python
import jax
import jax.numpy as jnp
from jax import lax
from jax.sharding import Mesh
from jax.sharding import PartitionSpec as P

BLK = 128
PROW = ("prow_0", "prow_1")
PCOL = ("pcol_0", "pcol_1")
PROW_PCOL = ("prow_0", "prow_1", "pcol_0", "pcol_1")


def laid_out(parts, dim):
    shape = list(parts.shape[1:])
    shape[dim] *= parts.shape[0]
    return jnp.moveaxis(parts, 0, dim).reshape(shape)


def stacked_from(x, axes, turns):
    parts = x[None]
    for k in turns:
        parts = lax.all_gather(parts, axes[k], axis=0, tiled=True)
    carried = [lax.axis_size(axes[k]) for k in reversed(turns)]
    parts = parts.reshape(*carried, *x.shape)
    turned = sorted(range(len(turns)), key=lambda place: turns[len(turns) - 1 - place])
    return parts.transpose(*turned, *range(len(turns), parts.ndim)).reshape(-1, *x.shape)


def whole_of(x, axes, turns, dim):
    return laid_out(stacked_from(x, axes, turns), dim)


def in_blocks(x, dim, count):
    shape = x.shape
    parts = x.reshape(*shape[:dim], count, shape[dim] // count, *shape[dim + 1 :])
    return jnp.moveaxis(parts, dim, 0)


def summed_on_arrival(x, axis, dim):
    count = lax.axis_size(axis)
    parts = lax.all_to_all(in_blocks(x, dim, count), axis, 0, 0, tiled=True)
    return jnp.sum(parts, axis=0)


def summed_rows(x, axes, dim):
    far, near = axes
    parts = in_blocks(x, dim, lax.axis_size(far))
    nearer = summed_on_arrival(parts, near, dim + 1)
    arrived = lax.all_to_all(nearer, far, split_axis=0, concat_axis=0, tiled=True)
    return arrived.sum(axis=0)


def rows_for(lines, count):
    spare = -lines.shape[0] % count
    if not spare:
        return lines
    return jnp.concatenate([lines, jnp.zeros((spare, *lines.shape[1:]), lines.dtype)])


def from_everyone(x, axis):
    copies = jnp.broadcast_to(x, (lax.axis_size(axis), *x.shape))
    return lax.all_to_all(copies, axis, split_axis=0, concat_axis=0, tiled=True)


def whole_of_2(x, axes, dim):
    far, near = axes
    leading = from_everyone(x, far)
    parts = jnp.swapaxes(from_everyone(leading, near), 0, 1)
    return laid_out(parts.reshape(-1, *x.shape), dim)


def nested_sum(x, axes):
    own = summed_rows(rows_for(x, lax.axis_size(axes[0]) * lax.axis_size(axes[1])), axes, 0)
    whole = whole_of_2(own, axes, 0)
    return whole[: len(x)].reshape(x.shape)


def together(arrays, axis):
    ends = [0]
    for a in arrays:
        ends.append(ends[-1] + a.size)
    total = nested_sum(jnp.concatenate([a.ravel() for a in arrays]), axis)
    return tuple((total[b:e].reshape(a.shape) for a, b, e in zip(arrays, ends, ends[1:])))


def product(left, right):
    return jnp.dot(left, right, precision=lax.Precision.HIGHEST, preferred_element_type=jnp.float32)


def transposed_product(left, right):
    return lax.dot_general(
        left,
        right,
        (((0,), (0,)), ((), ())),
        precision=lax.Precision.HIGHEST,
        preferred_element_type=jnp.float32,
    )


def live_rows(listing, first_row, count):
    row_ids = first_row + lax.iota(jnp.int32, count)
    blocks = row_ids // BLK
    hits = jnp.any(blocks[:, None] == listing[None, :], axis=1)
    return jnp.where(hits, 1.0, 0.0).astype(jnp.float32)[:, None]


def multiply_ancestors(inverse_tile, masked_span):
    groups = lax.axis_size(PROW) // lax.axis_size(PCOL)
    columns = lax.axis_size(PCOL)
    span_rows = masked_span.shape[0]
    stacked = whole_of(masked_span, PROW, (0, 1), 0)
    grouped = stacked.reshape(columns, groups * span_rows, masked_span.shape[1])
    regrouped = lax.all_to_all(grouped, PCOL, split_axis=0, concat_axis=0, tiled=True)
    accumulated = jnp.einsum(
        "rjkm,kjmw->rw",
        inverse_tile.reshape(inverse_tile.shape[0], groups, columns, span_rows),
        regrouped.reshape(columns, groups, span_rows, masked_span.shape[1]),
        precision=lax.Precision.HIGHEST,
        preferred_element_type=jnp.float32,
    )
    return summed_on_arrival(accumulated, PCOL, 0)


def local(inverse_pool, panel_one, panel_two, upper_two, lower_one, lower_two, list_one, list_two):
    span_rows = panel_one.shape[0]
    span_index = lax.axis_index(PROW) * lax.axis_size(PCOL) + lax.axis_index(PCOL)
    first_row = span_index * span_rows
    live_one = live_rows(list_one, first_row, span_rows)
    live_two = live_rows(list_two, first_row, span_rows)
    masked_one = live_one * panel_one
    masked_two = live_two * panel_two
    first_offdiag = -live_one * multiply_ancestors(inverse_pool, masked_one)
    second_product = multiply_ancestors(inverse_pool, masked_two)
    second_offdiag = -live_two * (product(first_offdiag, upper_two) + second_product)
    first_terms, coupling_terms, last_terms = together(
        (
            transposed_product(masked_one, first_offdiag),
            transposed_product(first_offdiag, masked_two),
            transposed_product(masked_two, second_offdiag),
        ),
        (("prow_0", "prow_1"), ("pcol_0", "pcol_1")),
    )
    first_diag = transposed_product(lower_one, lower_one) - first_terms
    second_coupling = -(product(first_diag, upper_two) + coupling_terms)
    second_diag = (
        transposed_product(lower_two, lower_two)
        - transposed_product(upper_two, second_coupling)
        - last_terms
    )
    return (first_offdiag, first_diag, second_offdiag, second_coupling, second_diag)


def solution(mesh):
    finer = Mesh(mesh.devices.reshape(4, 8, 4, 2), ("prow_0", "prow_1", "pcol_0", "pcol_1"))
    placed = (P(PROW, PCOL), P(PROW_PCOL, None), P(PROW_PCOL, None), P(), P(), P(), P(), P())
    return jax.shard_map(
        local,
        mesh=finer,
        in_specs=placed,
        out_specs=(P(PROW_PCOL, None), P(), P(PROW_PCOL, None), P(), P()),
        check_vma=False,
    )
```

profile of v0, /device:TPU:1, one launch (start us, length us, event | category | flops | bytes accessed | tf_op | source)
XLA Modules:
  0.0 368.6 jit_solution(7397864533906607054)
XLA Ops:
  9.8 12.3 %all-gather = f32[192,512]{1,0:T(8,128)} all-gather(f32[48,512]{1,0:T(8,128)S(1)} %broadcast_multiply_fusion.1), channel_id=2, replica_groups=mesh['prow_0'=4,'prow_1'=8,'pcol_0'=4,'pcol_1'=2] {'prow_0'}, dimensions={0}, use_global_device_ids=true | all-gather | bytes 491520 | tf_op jit(solution)/shard_map/all_gather | solution.py:22
  24.0 10.4 %all-gather.1 = f32[192,512]{1,0:T(8,128)} all-gather(f32[48,512]{1,0:T(8,128)S(1)} %broadcast_multiply_fusion), channel_id=3, replica_groups=mesh['prow_0'=4,'prow_1'=8,'pcol_0'=4,'pcol_1'=2] {'prow_0'}, dimensions={0}, use_global_device_ids=true | all-gather | bytes 491520 | tf_op jit(solution)/shard_map/all_gather | solution.py:22
  34.4 37.2 %all-gather.5.cloned.1.call-done = f32[32,48,512]{2,1,0:T(8,128)} async-done(((f32[4,48,512]{2,1,0:T(8,128)}), f32[32,48,512]{2,1,0:T(8,128)}) %all-gather.5.cloned.1.call-update) | async-done | bytes 3145744 | tf_op jit(solution)/shard_map/all_gather | solution.py:22
  71.6 4.1 %copy.41 = f32[4,8,48,512]{3,2,1,0:T(8,128)} copy(f32[4,8,48,512]{3,2,0,1:T(8,128)} %bitcast.75) | data formatting | bytes 6291456 | tf_op jit(solution)/shard_map/transpose | solution.py:26
  75.7 5.6 %all-to-all-start = ((f32[8,192,512]{2,1,0:T(8,128)}), f32[8,192,512]{2,1,0:T(8,128)}, u32[]{:S(2)}, u32[]{:S(2)}) async-start(f32[8,192,512]{2,1,0:T(8,128)} %bitcast.68), calls=%async_computation | async-start | bytes 6291456 | tf_op jit(solution)/shard_map/all_to_all | solution.py:113
  81.3 35.8 %all-gather.7.cloned.1.call-done = f32[32,48,512]{2,1,0:T(8,128)} async-done(((f32[4,48,512]{2,1,0:T(8,128)}), f32[32,48,512]{2,1,0:T(8,128)}) %all-gather.7.cloned.1.call-update) | async-done | bytes 3145744 | tf_op jit(solution)/shard_map/all_gather | solution.py:22
  117.1 4.0 %copy.44 = f32[4,8,48,512]{3,2,1,0:T(8,128)} copy(f32[4,8,48,512]{3,2,0,1:T(8,128)} %bitcast.76) | data formatting | bytes 6291456 | tf_op jit(solution)/shard_map/transpose | solution.py:26
  121.1 5.6 %all-to-all-start.2 = ((f32[8,192,512]{2,1,0:T(8,128)}), f32[8,192,512]{2,1,0:T(8,128)}, u32[]{:S(2)}, u32[]{:S(2)}) async-start(f32[8,192,512]{2,1,0:T(8,128)} %bitcast.67), calls=%async_computation.2 | async-start | bytes 6291456 | tf_op jit(solution)/shard_map/all_to_all | solution.py:113
  126.7 2.0 copy.42
  128.7 6.8 %fusion.2 = f32[512,384,1,1]{0,1,3,2:T(8,128)} fusion(f32[384,4,8,48]{0,3,2,1:T(8,128)S(1)} %bitcast.65, f32[8,4,48,512]{3,2,1,0:T(8,128)} %bitcast.4), kind=kOutput, calls=%fused_computation.3 | convolution fusion | flops 3623878656 | bytes 6291456 | tf_op jit(solution)/shard_map/rjkm,kjmw->rw/dot_general | solution.py:114
  135.5 28.8 %all-to-all-done.2 = f32[8,192,512]{2,1,0:T(8,128)} async-done(((f32[8,192,512]{2,1,0:T(8,128)}), f32[8,192,512]{2,1,0:T(8,128)}, u32[]{:S(2)}, u32[]{:S(2)}) %all-to-all-start.2) | async-done | bytes 3145760 | tf_op jit(solution)/shard_map/all_to_all | solution.py:113
  164.2 5.1 %all-to-all-start.1 = ((f32[8,48,512]{2,1,0:T(8,128)}), f32[8,48,512]{2,1,0:T(8,128)}, u32[]{:S(2)}, u32[]{:S(2)}) async-start(f32[8,48,512]{2,1,0:T(8,128)} %bitcast.74), calls=%async_computation.1 | async-start | bytes 1572864 | tf_op jit(solution)/shard_map/all_to_all | solution.py:41
  169.3 6.8 %fusion = f32[512,384,1,1]{0,1,3,2:T(8,128)} fusion(f32[384,4,8,48]{0,3,2,1:T(8,128)S(1)} %bitcast.66, f32[8,4,48,512]{3,2,1,0:T(8,128)} %bitcast.14), kind=kOutput, calls=%fused_computation.1 | convolution fusion | flops 3623878656 | bytes 6291456 | tf_op jit(solution)/shard_map/rjkm,kjmw->rw/dot_general | solution.py:114
  176.1 5.5 %all-to-all-done.1 = f32[8,48,512]{2,1,0:T(8,128)} async-done(((f32[8,48,512]{2,1,0:T(8,128)}), f32[8,48,512]{2,1,0:T(8,128)}, u32[]{:S(2)}, u32[]{:S(2)}) %all-to-all-start.1) | async-done | bytes 786464 | tf_op jit(solution)/shard_map/all_to_all | solution.py:41
  181.6 5.1 %all-to-all-start.3 = ((f32[8,48,512]{2,1,0:T(8,128)}), f32[8,48,512]{2,1,0:T(8,128)}, u32[]{:S(2)}, u32[]{:S(2)}) async-start(f32[8,48,512]{2,1,0:T(8,128)} %bitcast.73), calls=%async_computation.3 | async-start | bytes 1572864 | tf_op jit(solution)/shard_map/all_to_all | solution.py:41
  190.0 8.9 %all-to-all-done.3 = f32[8,48,512]{2,1,0:T(8,128)} async-done(((f32[8,48,512]{2,1,0:T(8,128)}), f32[8,48,512]{2,1,0:T(8,128)}, u32[]{:S(2)}, u32[]{:S(2)}) %all-to-all-start.3) | async-done | bytes 786464 | tf_op jit(solution)/shard_map/all_to_all | solution.py:41
  204.3 1.8 pad_maximum_fusion
  206.2 4.5 %reshape_reshape.4 = f32[32,8,3072]{2,1,0:T(8,128)} reshape(f32[786432]{0:T(1024)} %pad_maximum_fusion) | data formatting | bytes 6291456 | tf_op jit(solution)/shard_map/reshape;reshape | solution.py:35
  210.7 3.7 %copy.46 = f32[8,32,3072]{2,1,0:T(8,128)S(1)} copy(f32[8,32,3072]{2,0,1:T(8,128)} %bitcast.69) | data formatting | bytes 6291456 | tf_op jit(solution)/shard_map/transpose | solution.py:36
  214.4 41.6 %all_to_all.48 = f32[8,32,3072]{2,1,0:T(8,128)} all-to-all(f32[8,32,3072]{2,1,0:T(8,128)S(1)} %copy.46), channel_id=1, replica_groups=mesh['prow_0'=4,'prow_1'=8,'pcol_0'=4,'pcol_1'=2] {'pcol_0','pcol_1'}, dimensions={0} | all-to-all | bytes 6291456 | tf_op jit(solution)/shard_map/all_to_all | solution.py:41
  256.0 2.1 reduce_sum.38
  258.3 17.6 %all_to_all.49 = f32[32,1,3072]{2,1,0:T(1,128)S(1)} all-to-all(f32[32,1,3072]{2,1,0:T(1,128)S(1)} %all_to_all.35), channel_id=1, replica_groups=mesh['prow_0'=4,'prow_1'=8,'pcol_0'=4,'pcol_1'=2] {'prow_0','prow_1'}, dimensions={0} | all-to-all | bytes 786432 | tf_op jit(solution)/shard_map/all_to_all | solution.py:49
  276.4 18.1 %all_to_all.50 = f32[32,1,3072]{2,1,0:T(1,128)S(1)} all-to-all(f32[32,1,3072]{2,1,0:T(1,128)S(1)} %broadcast_in_dim.32), channel_id=1, replica_groups=mesh['prow_0'=4,'prow_1'=8,'pcol_0'=4,'pcol_1'=2] {'prow_0','prow_1'}, dimensions={0} | all-to-all | bytes 786432 | tf_op jit(solution)/shard_map/all_to_all | solution.py:62
  294.6 2.0 broadcast_in_dim.33
  296.6 9.4 %all-to-all-start.7 = ((f32[8,32,3072]{2,1,0:T(8,128)}), f32[8,32,3072]{2,1,0:T(8,128)}, u32[]{:S(2)}, u32[]{:S(2)}) async-start(f32[8,32,3072]{2,1,0:T(8,128)} %broadcast_in_dim.33), calls=%async_computation.7 | async-start | bytes 6291456 | tf_op jit(solution)/shard_map/all_to_all | solution.py:62
  306.0 1.9 fusion.10
  307.9 35.7 %all-to-all-done.7 = f32[8,32,3072]{2,1,0:T(8,128)} async-done(((f32[8,32,3072]{2,1,0:T(8,128)}), f32[8,32,3072]{2,1,0:T(8,128)}, u32[]{:S(2)}, u32[]{:S(2)}) %all-to-all-start.7) | async-done | bytes 3145760 | tf_op jit(solution)/shard_map/all_to_all | solution.py:62
  343.6 5.4 %copy.47 = f32[32,8,3072]{2,1,0:T(8,128)} copy(f32[32,8,3072]{2,0,1:T(8,128)} %bitcast.20) | data formatting | bytes 6291456 | tf_op jit(solution)/shard_map/transpose | solution.py:68
  349.0 4.7 %slice.14 = f32[1536,512]{1,0:T(8,128)} reshape(f32[32,8,3072]{2,1,0:T(8,128)} %copy.47) | data formatting | bytes 6291456 | tf_op jit(solution)/shard_map/slice | solution.py:83
  353.7 3.3 convolution_subtract_fusion
  357.0 1.9 fusion.6
  358.9 2.9 fusion.5
  (46 shorter events, 13.9 us)
Async XLA Ops:
  7.2 193.6 %copy-start = (f32[512,512]{1,0:T(8,128)S(1)}, f32[512,512]{1,0:T(8,128)}, u32[]{:S(2)}) copy-start(f32[512,512]{1,0:T(8,128)} %param.11) | copy-start | bytes 3145732
  7.2 64.5 %all-gather.5.cloned.1.call-start = ((), (), s32[]{:S(2)}) async-start(), calls=%async_computation.8 | async-start | bytes 3538944 | tf_op jit(solution)/shard_map/all_gather | solution.py:22
  9.2 0.6 copy-start.7
  22.1 95.0 %all-gather.7.cloned.1.call-start = ((), (), s32[]{:S(2)}) async-start(), calls=%async_computation.9 | async-start | bytes 3538944 | tf_op jit(solution)/shard_map/all_gather | solution.py:22
  75.7 45.4 %all-to-all-start = ((f32[8,192,512]{2,1,0:T(8,128)}), f32[8,192,512]{2,1,0:T(8,128)}, u32[]{:S(2)}, u32[]{:S(2)}) async-start(f32[8,192,512]{2,1,0:T(8,128)} %bitcast.68), calls=%async_computation | async-start | bytes 6291456 | tf_op jit(solution)/shard_map/all_to_all | solution.py:113
  121.1 43.1 %all-to-all-start.2 = ((f32[8,192,512]{2,1,0:T(8,128)}), f32[8,192,512]{2,1,0:T(8,128)}, u32[]{:S(2)}, u32[]{:S(2)}) async-start(f32[8,192,512]{2,1,0:T(8,128)} %bitcast.67), calls=%async_computation.2 | async-start | bytes 6291456 | tf_op jit(solution)/shard_map/all_to_all | solution.py:113
  164.2 17.4 %all-to-all-start.1 = ((f32[8,48,512]{2,1,0:T(8,128)}), f32[8,48,512]{2,1,0:T(8,128)}, u32[]{:S(2)}, u32[]{:S(2)}) async-start(f32[8,48,512]{2,1,0:T(8,128)} %bitcast.74), calls=%async_computation.1 | async-start | bytes 1572864 | tf_op jit(solution)/shard_map/all_to_all | solution.py:41
  176.1 12.9 %copy-start.8 = (f32[48,512]{1,0:T(8,128)S(1)}, f32[48,512]{1,0:T(8,128)}, u32[]{:S(2)}) copy-start(f32[48,512]{1,0:T(8,128)} %copy-done.7) | copy-start | bytes 294916
  181.6 17.4 %all-to-all-start.3 = ((f32[8,48,512]{2,1,0:T(8,128)}), f32[8,48,512]{2,1,0:T(8,128)}, u32[]{:S(2)}, u32[]{:S(2)}) async-start(f32[8,48,512]{2,1,0:T(8,128)} %bitcast.73), calls=%async_computation.3 | async-start | bytes 1572864 | tf_op jit(solution)/shard_map/all_to_all | solution.py:41
  187.9 15.8 %copy-start.6 = (f32[48,512]{1,0:T(8,128)}, f32[48,512]{1,0:T(8,128)S(1)}, u32[]{:S(2)}) copy-start(f32[48,512]{1,0:T(8,128)S(1)} %broadcast_multiply_fusion.2) | copy-start | bytes 294916
  202.4 1.9 copy-start.9
  296.6 9.4 %copy-start.2 = (f32[512,512]{1,0:T(8,128)S(1)}, f32[512,512]{1,0:T(8,128)}, u32[]{:S(2)}) copy-start(f32[512,512]{1,0:T(8,128)} %param.13) | copy-start | bytes 3145732
  296.6 47.0 %all-to-all-start.7 = ((f32[8,32,3072]{2,1,0:T(8,128)}), f32[8,32,3072]{2,1,0:T(8,128)}, u32[]{:S(2)}, u32[]{:S(2)}) async-start(f32[8,32,3072]{2,1,0:T(8,128)} %broadcast_in_dim.33), calls=%async_computation.7 | async-start | bytes 6291456 | tf_op jit(solution)/shard_map/all_to_all | solution.py:62
  349.0 4.7 %copy-start.3 = (f32[512,512]{1,0:T(8,128)S(1)}, f32[512,512]{1,0:T(8,128)}, u32[]{:S(2)}) copy-start(f32[512,512]{1,0:T(8,128)} %param.12) | copy-start | bytes 3145732
  353.7 3.3 copy-start.1
  357.0 4.8 %copy-start.5 = (f32[512,512]{1,0:T(8,128)}, f32[512,512]{1,0:T(8,128)S(1)}, u32[]{:S(2)}) copy-start(f32[512,512]{1,0:T(8,128)S(1)} %convolution_subtract_fusion) | copy-start | bytes 3145732
  358.8 2.9 copy-start.4
Sparse Core Ops, SparseCore 0:
  22.2 49.3 all-gather.4
  73.4 43.5 all-gather.6
where the time goes:
time: 370 us; the launch traced here: 369 us
  waiting for transfers between devices  152 us (41%)
  blocking collectives  100 us (27%)
  local copies, waits for them, and re-layouts  32.6 us (9%)
  starting transfers between devices  30.7 us (8%)
  matrix products  28 us (8%)
  between operations  14.3 us (4%)
  other arithmetic  11 us (3%)
    all_gather x2, waiting for transfers between devices, stacked_from(): parts = lax.all_gather(parts, axes[k], axis=0, tiled=True)  73 us
    all_to_all x1, blocking collectives, summed_on_arrival(): parts = lax.all_to_all(in_blocks(x, dim, count), axis, 0, 0, tiled=True)  41.6 us
    all_to_all x1, waiting for transfers between devices, from_everyone(): return lax.all_to_all(copies, axis, split_axis=0, concat_axis=0, tiled=True)  35.7 us
    all_to_all x2, waiting for transfers between devices, multiply_ancestors(): lax.all_to_all(grouped, PCOL, split_axis=0, concat_axis=0, tiled=True)  28.8 us
    all_gather x2, blocking collectives, stacked_from(): parts = lax.all_gather(parts, axes[k], axis=0, tiled=True)  22.7 us
    all_to_all x1, blocking collectives, from_everyone(): return lax.all_to_all(copies, axis, split_axis=0, concat_axis=0, tiled=True)  18.1 us
    all_to_all x1, blocking collectives, summed_rows(): lax.all_to_all(nearer, far, split_axis=0, concat_axis=0, tiled=True)  17.6 us
    all_to_all x2, waiting for transfers between devices, summed_on_arrival(): parts = lax.all_to_all(in_blocks(x, dim, count), axis, 0, 0, tiled=True)  14.5 us
  transfers between devices with their start and end apart: 7, of which 6 were waited for; matrix products, arithmetic and copies ran while one was open for 8% of the time, Pallas kernels for 0%

commit v1 on v0

--- a/solution.py
+++ b/solution.py
@@ -10,6 +10,13 @@
 PROW_PCOL = ("prow_0", "prow_1", "pcol_0", "pcol_1")
 
 
+def all_by_exchange(block, axis, dim):
+    size = lax.axis_size(axis)
+    blocks = jnp.stack([block for _ in range(size)])
+    blocks = lax.all_to_all(blocks, axis, split_axis=0, concat_axis=0)
+    return jnp.concatenate(blocks, axis=dim)
+
+
 def laid_out(parts, dim):
     shape = list(parts.shape[1:])
     shape[dim] *= parts.shape[0]
@@ -19,7 +26,7 @@
 def stacked_from(x, axes, turns):
     parts = x[None]
     for k in turns:
-        parts = lax.all_gather(parts, axes[k], axis=0, tiled=True)
+        parts = all_by_exchange(parts, axes[k], 0)
     carried = [lax.axis_size(axes[k]) for k in reversed(turns)]
     parts = parts.reshape(*carried, *x.shape)
     turned = sorted(range(len(turns)), key=lambda place: turns[len(turns) - 1 - place])

time: 370 us -> 464 us (1.25)
  blocking collectives: 100 us -> 161 us
  waiting for transfers between devices: 152 us -> 182 us
  between operations: 14.3 us -> 0.9 us
  starting transfers between devices: 30.7 us -> 44 us
    all_to_all x0 -> x2, blocking collectives: none -> 86.7 us  [all_by_exchange(): blocks = lax.all_to_all(blocks, axis, split_axis=0, concat_axis=0)]
    all_gather x2 -> x0, waiting for transfers between devices: 73 us -> none  [stacked_from(): parts = lax.all_gather(parts, axes[k], axis=0, tiled=True)]
    all_to_all x0 -> x2, waiting for transfers between devices: none -> 69.2 us  [all_by_exchange(): blocks = lax.all_to_all(blocks, axis, split_axis=0, concat_axis=0)]
    all_to_all x2, waiting for transfers between devices: 28.8 us -> 62.3 us  [multiply_ancestors(): lax.all_to_all(grouped, PCOL, split_axis=0, concat_axis=0, tiled=True)]
    all_gather x2 -> x0, blocking collectives: 22.7 us -> none  [stacked_from(): parts = lax.all_gather(parts, axes[k], axis=0, tiled=True)]
    all_to_all x0 -> x2, starting transfers between devices: none -> 9.27 us  [all_by_exchange(): blocks = lax.all_to_all(blocks, axis, split_axis=0, concat_axis=0)]
    transpose x2 -> x0, local copies, waits for them, and re-layouts: 8.14 us -> none  [stacked_from(): parts.transpose(*turned, *range(len(turns), parts.ndim))]
    all_to_all x0 -> x2, local copies, waits for them, and re-layouts: none -> 8.1 us  [all_by_exchange(): blocks = lax.all_to_all(blocks, axis, split_axis=0, concat_axis=0)]
  transfers between devices with their start and end apart: 7 -> 7, of which waited for: 6 -> 7; matrix products, arithmetic and copies ran while one was open for 8% -> 7% of each run, Pallas kernels for 0% -> 0%
where the time goes in v1:
time: 464 us; the launch traced here: 462 us
  waiting for transfers between devices  182 us (39%)
  blocking collectives  161 us (35%)
  starting transfers between devices  44 us (9%)
  local copies, waits for them, and re-layouts  35.8 us (8%)
  matrix products  28 us (6%)
  other arithmetic  11 us (2%)
    all_to_all x2, blocking collectives, all_by_exchange(): blocks = lax.all_to_all(blocks, axis, split_axis=0, concat_axis=0)  86.7 us
    all_to_all x2, waiting for transfers between devices, all_by_exchange(): blocks = lax.all_to_all(blocks, axis, split_axis=0, concat_axis=0)  69.2 us
    all_to_all x2, waiting for transfers between devices, multiply_ancestors(): lax.all_to_all(grouped, PCOL, split_axis=0, concat_axis=0, tiled=True)  62.3 us
    all_to_all x1, blocking collectives, summed_on_arrival(): parts = lax.all_to_all(in_blocks(x, dim, count), axis, 0, 0, tiled=True)  41.6 us
    all_to_all x1, waiting for transfers between devices, from_everyone(): return lax.all_to_all(copies, axis, split_axis=0, concat_axis=0, tiled=True)  35.7 us
    all_to_all x1, blocking collectives, from_everyone(): return lax.all_to_all(copies, axis, split_axis=0, concat_axis=0, tiled=True)  18.1 us
    all_to_all x2, starting transfers between devices, multiply_ancestors(): lax.all_to_all(grouped, PCOL, split_axis=0, concat_axis=0, tiled=True)  15.6 us
    all_to_all x1, blocking collectives, summed_rows(): lax.all_to_all(nearer, far, split_axis=0, concat_axis=0, tiled=True)  14.6 us
  transfers between devices with their start and end apart: 7, of which 7 were waited for; matrix products, arithmetic and copies ran while one was open for 7% of the time, Pallas kernels for 0%

profile of v1, /device:TPU:1, one launch (start us, length us, event | category | flops | bytes accessed | tf_op | source)
XLA Modules:
  0.0 462.3 jit_solution(5653758553585730392)
XLA Ops:
  4.0 4.8 %all-to-all-start = ((f32[4,1,48,512]{3,2,1,0:T(8,128)}), f32[4,1,48,512]{3,2,1,0:T(8,128)S(1)}, u32[]{:S(2)}, u32[]{:S(2)}) async-start(f32[4,1,48,512]{3,2,1,0:T(8,128)} %stack.12), calls=%async_computation | async-start | bytes 786432 | tf_op jit(solution)/shard_map/all_to_all | solution.py:16
  10.7 4.4 all-to-all-done
  15.1 8.6 %all_to_all.68 = f32[4,1,48,512]{3,2,1,0:T(8,128)S(1)} all-to-all(f32[4,1,48,512]{3,2,1,0:T(8,128)S(1)} %stack.14), channel_id=1, replica_groups=mesh['prow_0'=4,'prow_1'=8,'pcol_0'=4,'pcol_1'=2] {'prow_0'}, dimensions={0} | all-to-all | bytes 786432 | tf_op jit(solution)/shard_map/all_to_all | solution.py:16
  24.1 78.1 %all_to_all.69 = f32[8,4,48,512]{3,2,1,0:T(8,128)} all-to-all(f32[8,4,48,512]{3,2,1,0:T(8,128)S(1)} %stack.13), channel_id=1, replica_groups=mesh['prow_0'=4,'prow_1'=8,'pcol_0'=4,'pcol_1'=2] {'prow_1'}, dimensions={0} | all-to-all | bytes 6291456 | tf_op jit(solution)/shard_map/all_to_all | solution.py:16
  102.2 2.0 stack.15
  104.3 4.4 all-to-all-start.5
  108.7 4.1 copy.35
  112.8 64.8 %all-to-all-done.5 = f32[8,4,48,512]{3,2,1,0:T(8,128)} async-done(((f32[8,4,48,512]{3,2,1,0:T(8,128)}), f32[8,4,48,512]{3,2,1,0:T(8,128)}, u32[]{:S(2)}, u32[]{:S(2)}) %all-to-all-start.5) | async-done | bytes 3145760 | tf_op jit(solution)/shard_map/all_to_all | solution.py:16
  177.5 10.3 %all-to-all-start.2 = ((f32[8,192,512]{2,1,0:T(8,128)}), f32[8,192,512]{2,1,0:T(8,128)}, u32[]{:S(2)}, u32[]{:S(2)}) async-start(f32[8,192,512]{2,1,0:T(8,128)} %bitcast.66), calls=%async_computation.2 | async-start | bytes 6291456 | tf_op jit(solution)/shard_map/all_to_all | solution.py:120
  187.8 4.0 copy.38
  191.9 33.5 %all-to-all-done.2 = f32[8,192,512]{2,1,0:T(8,128)} async-done(((f32[8,192,512]{2,1,0:T(8,128)}), f32[8,192,512]{2,1,0:T(8,128)}, u32[]{:S(2)}, u32[]{:S(2)}) %all-to-all-start.2) | async-done | bytes 3145760 | tf_op jit(solution)/shard_map/all_to_all | solution.py:120
  225.4 5.3 %all-to-all-start.6 = ((f32[8,192,512]{2,1,0:T(8,128)}), f32[8,192,512]{2,1,0:T(8,128)}, u32[]{:S(2)}, u32[]{:S(2)}) async-start(f32[8,192,512]{2,1,0:T(8,128)} %bitcast.65), calls=%async_computation.6 | async-start | bytes 6291456 | tf_op jit(solution)/shard_map/all_to_all | solution.py:120
  232.7 6.8 %fusion.2 = f32[512,384,1,1]{0,1,3,2:T(8,128)} fusion(f32[384,4,8,48]{0,3,2,1:T(8,128)S(1)} %bitcast.63, f32[8,4,48,512]{3,2,1,0:T(8,128)} %bitcast.3), kind=kOutput, calls=%fused_computation.3 | convolution fusion | flops 3623878656 | bytes 6291456 | tf_op jit(solution)/shard_map/rjkm,kjmw->rw/dot_general | solution.py:121
  239.5 28.8 %all-to-all-done.6 = f32[8,192,512]{2,1,0:T(8,128)} async-done(((f32[8,192,512]{2,1,0:T(8,128)}), f32[8,192,512]{2,1,0:T(8,128)}, u32[]{:S(2)}, u32[]{:S(2)}) %all-to-all-start.6) | async-done | bytes 3145760 | tf_op jit(solution)/shard_map/all_to_all | solution.py:120
  268.2 5.1 %all-to-all-start.3 = ((f32[8,48,512]{2,1,0:T(8,128)}), f32[8,48,512]{2,1,0:T(8,128)}, u32[]{:S(2)}, u32[]{:S(2)}) async-start(f32[8,48,512]{2,1,0:T(8,128)} %bitcast.72), calls=%async_computation.3 | async-start | bytes 1572864 | tf_op jit(solution)/shard_map/all_to_all | solution.py:48
  273.3 6.8 %fusion = f32[512,384,1,1]{0,1,3,2:T(8,128)} fusion(f32[384,4,8,48]{0,3,2,1:T(8,128)S(1)} %bitcast.64, f32[8,4,48,512]{3,2,1,0:T(8,128)} %bitcast.12), kind=kOutput, calls=%fused_computation.1 | convolution fusion | flops 3623878656 | bytes 6291456 | tf_op jit(solution)/shard_map/rjkm,kjmw->rw/dot_general | solution.py:121
  280.0 5.5 %all-to-all-done.3 = f32[8,48,512]{2,1,0:T(8,128)} async-done(((f32[8,48,512]{2,1,0:T(8,128)}), f32[8,48,512]{2,1,0:T(8,128)}, u32[]{:S(2)}, u32[]{:S(2)}) %all-to-all-start.3) | async-done | bytes 786464 | tf_op jit(solution)/shard_map/all_to_all | solution.py:48
  285.6 5.1 %all-to-all-start.7 = ((f32[8,48,512]{2,1,0:T(8,128)}), f32[8,48,512]{2,1,0:T(8,128)}, u32[]{:S(2)}, u32[]{:S(2)}) async-start(f32[8,48,512]{2,1,0:T(8,128)} %bitcast.71), calls=%async_computation.7 | async-start | bytes 1572864 | tf_op jit(solution)/shard_map/all_to_all | solution.py:48
  294.0 8.9 %all-to-all-done.7 = f32[8,48,512]{2,1,0:T(8,128)} async-done(((f32[8,48,512]{2,1,0:T(8,128)}), f32[8,48,512]{2,1,0:T(8,128)}, u32[]{:S(2)}, u32[]{:S(2)}) %all-to-all-start.7) | async-done | bytes 786464 | tf_op jit(solution)/shard_map/all_to_all | solution.py:48
  310.1 4.5 reshape_reshape.4
  314.7 3.7 copy.40
  318.4 41.6 %all_to_all.70 = f32[8,32,3072]{2,1,0:T(8,128)} all-to-all(f32[8,32,3072]{2,1,0:T(8,128)S(1)} %copy.40), channel_id=1, replica_groups=mesh['prow_0'=4,'prow_1'=8,'pcol_0'=4,'pcol_1'=2] {'pcol_0','pcol_1'}, dimensions={0} | all-to-all | bytes 6291456 | tf_op jit(solution)/shard_map/all_to_all | solution.py:48
  360.0 2.1 reduce_sum.38
  362.3 14.6 %all_to_all.71 = f32[32,1,3072]{2,1,0:T(1,128)S(1)} all-to-all(f32[32,1,3072]{2,1,0:T(1,128)S(1)} %all_to_all.51), channel_id=1, replica_groups=mesh['prow_0'=4,'prow_1'=8,'pcol_0'=4,'pcol_1'=2] {'prow_0','prow_1'}, dimensions={0} | all-to-all | bytes 786432 | tf_op jit(solution)/shard_map/all_to_all | solution.py:56
  377.3 18.1 %all_to_all.72 = f32[32,1,3072]{2,1,0:T(1,128)S(1)} all-to-all(f32[32,1,3072]{2,1,0:T(1,128)S(1)} %broadcast_in_dim.24), channel_id=1, replica_groups=mesh['prow_0'=4,'prow_1'=8,'pcol_0'=4,'pcol_1'=2] {'prow_0','prow_1'}, dimensions={0} | all-to-all | bytes 786432 | tf_op jit(solution)/shard_map/all_to_all | solution.py:69
  395.5 2.0 broadcast_in_dim.25
  397.6 9.1 %all-to-all-start.11 = ((f32[8,32,3072]{2,1,0:T(8,128)}), f32[8,32,3072]{2,1,0:T(8,128)}, u32[]{:S(2)}, u32[]{:S(2)}) async-start(f32[8,32,3072]{2,1,0:T(8,128)} %broadcast_in_dim.25), calls=%async_computation.11 | async-start | bytes 6291456 | tf_op jit(solution)/shard_map/all_to_all | solution.py:69
  408.5 35.7 %all-to-all-done.11 = f32[8,32,3072]{2,1,0:T(8,128)} async-done(((f32[8,32,3072]{2,1,0:T(8,128)}), f32[8,32,3072]{2,1,0:T(8,128)}, u32[]{:S(2)}, u32[]{:S(2)}) %all-to-all-start.11) | async-done | bytes 3145760 | tf_op jit(solution)/shard_map/all_to_all | solution.py:69
  444.2 5.4 %copy.41 = f32[32,8,3072]{2,1,0:T(8,128)} copy(f32[32,8,3072]{2,0,1:T(8,128)} %bitcast.18) | data formatting | bytes 6291456 | tf_op jit(solution)/shard_map/transpose | solution.py:75
  449.6 4.7 %slice.14 = f32[1536,512]{1,0:T(8,128)} reshape(f32[32,8,3072]{2,1,0:T(8,128)} %copy.41) | data formatting | bytes 6291456 | tf_op jit(solution)/shard_map/slice | solution.py:90
  454.3 3.3 convolution_subtract_fusion
  459.5 2.9 fusion.5
  (48 shorter events, 22.6 us)
Async XLA Ops:
  0.6 304.1 %copy-start = (f32[512,512]{1,0:T(8,128)S(1)}, f32[512,512]{1,0:T(8,128)}, u32[]{:S(2)}) copy-start(f32[512,512]{1,0:T(8,128)} %param.11) | copy-start | bytes 3145732
  2.6 0.6 copy-start.7
  4.0 11.1 %all-to-all-start = ((f32[4,1,48,512]{3,2,1,0:T(8,128)}), f32[4,1,48,512]{3,2,1,0:T(8,128)S(1)}, u32[]{:S(2)}, u32[]{:S(2)}) async-start(f32[4,1,48,512]{3,2,1,0:T(8,128)} %stack.12), calls=%async_computation | async-start | bytes 786432 | tf_op jit(solution)/shard_map/all_to_all | solution.py:16
  104.3 73.3 %all-to-all-start.5 = ((f32[8,4,48,512]{3,2,1,0:T(8,128)}), f32[8,4,48,512]{3,2,1,0:T(8,128)}, u32[]{:S(2)}, u32[]{:S(2)}) async-start(f32[8,4,48,512]{3,2,1,0:T(8,128)} %stack.15), calls=%async_computation.5 | async-start | bytes 6291456 | tf_op jit(solution)/shard_map/all_to_all | solution.py:16
  177.5 47.8 %all-to-all-start.2 = ((f32[8,192,512]{2,1,0:T(8,128)}), f32[8,192,512]{2,1,0:T(8,128)}, u32[]{:S(2)}, u32[]{:S(2)}) async-start(f32[8,192,512]{2,1,0:T(8,128)} %bitcast.66), calls=%async_computation.2 | async-start | bytes 6291456 | tf_op jit(solution)/shard_map/all_to_all | solution.py:120
  225.4 42.9 %all-to-all-start.6 = ((f32[8,192,512]{2,1,0:T(8,128)}), f32[8,192,512]{2,1,0:T(8,128)}, u32[]{:S(2)}, u32[]{:S(2)}) async-start(f32[8,192,512]{2,1,0:T(8,128)} %bitcast.65), calls=%async_computation.6 | async-start | bytes 6291456 | tf_op jit(solution)/shard_map/all_to_all | solution.py:120
  268.2 17.4 %all-to-all-start.3 = ((f32[8,48,512]{2,1,0:T(8,128)}), f32[8,48,512]{2,1,0:T(8,128)}, u32[]{:S(2)}, u32[]{:S(2)}) async-start(f32[8,48,512]{2,1,0:T(8,128)} %bitcast.72), calls=%async_computation.3 | async-start | bytes 1572864 | tf_op jit(solution)/shard_map/all_to_all | solution.py:48
  280.0 12.9 %copy-start.8 = (f32[48,512]{1,0:T(8,128)S(1)}, f32[48,512]{1,0:T(8,128)}, u32[]{:S(2)}) copy-start(f32[48,512]{1,0:T(8,128)} %copy-done.7) | copy-start | bytes 294916
  285.6 17.3 %all-to-all-start.7 = ((f32[8,48,512]{2,1,0:T(8,128)}), f32[8,48,512]{2,1,0:T(8,128)}, u32[]{:S(2)}, u32[]{:S(2)}) async-start(f32[8,48,512]{2,1,0:T(8,128)} %bitcast.71), calls=%async_computation.7 | async-start | bytes 1572864 | tf_op jit(solution)/shard_map/all_to_all | solution.py:48
  291.9 15.8 %copy-start.6 = (f32[48,512]{1,0:T(8,128)}, f32[48,512]{1,0:T(8,128)S(1)}, u32[]{:S(2)}) copy-start(f32[48,512]{1,0:T(8,128)S(1)} %broadcast_multiply_fusion.2) | copy-start | bytes 294916
  306.4 1.9 copy-start.9
  397.6 9.1 %copy-start.2 = (f32[512,512]{1,0:T(8,128)S(1)}, f32[512,512]{1,0:T(8,128)}, u32[]{:S(2)}) copy-start(f32[512,512]{1,0:T(8,128)} %param.13) | copy-start | bytes 3145732
  397.6 46.6 %all-to-all-start.11 = ((f32[8,32,3072]{2,1,0:T(8,128)}), f32[8,32,3072]{2,1,0:T(8,128)}, u32[]{:S(2)}, u32[]{:S(2)}) async-start(f32[8,32,3072]{2,1,0:T(8,128)} %broadcast_in_dim.25), calls=%async_computation.11 | async-start | bytes 6291456 | tf_op jit(solution)/shard_map/all_to_all | solution.py:69
  449.6 4.7 %copy-start.3 = (f32[512,512]{1,0:T(8,128)S(1)}, f32[512,512]{1,0:T(8,128)}, u32[]{:S(2)}) copy-start(f32[512,512]{1,0:T(8,128)} %param.12) | copy-start | bytes 3145732
  454.3 3.3 copy-start.1
  457.6 4.8 %copy-start.5 = (f32[512,512]{1,0:T(8,128)}, f32[512,512]{1,0:T(8,128)S(1)}, u32[]{:S(2)}) copy-start(f32[512,512]{1,0:T(8,128)S(1)} %convolution_subtract_fusion) | copy-start | bytes 3145732
  459.5 2.9 copy-start.4
